TPU v7x, 32 devices: a whole 2x2x4 slice. The times are simulated.
32 devices in a mesh: groups: 2 (over y), kvb: 4 (over z), tp: 4 (over x, core).
Axes of the slice: x: 2, y: 2, z: 4, core: 2. Of those that a mesh axis runs over, the one named last changes fastest.
Arguments:
- residual: bfloat16 [32, 8192], P(('groups', 'kvb')), parts along dimension 0, may hold values from -3 to 3
- queries: bfloat16 [32, 8192], P(('groups', 'kvb'), 'tp'), parts along dimension 0, may hold values from -60 to 60
- new_kv: bfloat16 [32, 2048], P(('groups', 'kvb')), parts along dimension 0, may hold values from -6 to 6
- kv_cache: bfloat16 [2048, 16, 2048], P(('groups', 'kvb', 'tp')), parts along dimension 0, may hold values from -6 to 6
- lengths: int32 [32], P('groups'), parts along dimension 0, may hold values from 1 to 2048, as said below
- slot_seq: int32 [2048], P(('groups', 'kvb', 'tp')), parts along dimension 0, may hold values from 0 to 15, as said below
- slot_block: int32 [2048], P(('groups', 'kvb', 'tp')), parts along dimension 0, may hold values from 0 to 127, as said below
- block_counts: int32 [32], P(('groups', 'kvb', 'tp')), parts along dimension 0, may hold values from 16 to 64, as said below
- out_weight: bfloat16 [8192, 8192], P('tp'), may hold values from -0.5 to 0.5
- norm_gain: bfloat16 [8192], P('tp'), may hold values from 0.099609375 to 1.8984375
Outputs:
- stream: bfloat16 [32, 8192], P(('groups', 'kvb'), 'tp'), parts along dimension 0
- normed: bfloat16 [32, 8192], P(('groups', 'kvb'), 'tp'), parts along dimension 0
There are 2 independent parts, one for each index of `groups`. A program takes and returns all parts, laid end to end along the dimension named above; an argument that names none is the same for every part. Nothing has to cross between parts.
Inputs may be any that keep to these rules, and one draw needn't show every extreme that they name: `block_counts`: slots below a device's count hold cache blocks, those at or beyond it none; at least one device's count is 64. `slot_seq`: each pair of a sequence s and a block b below ceil(lengths[s] / 16) sits in exactly one live slot of the group. `slot_block`: some sequence has exactly 128 blocks; none has more. `lengths`: some sequence has exactly 16 * (128) tokens.
All inputs are finite; a program needn't handle non-finite values.
Results may differ from a plain program's by a relative error of at most 0.006.
Values may be sent and summed in bfloat16 or wider, within the bound.
A program may use at most 64 MiB of HBM per device.

v0:
```python
import math

import jax
import jax.numpy as jnp
from jax import lax
from jax.experimental import pallas as pl
from jax.experimental.pallas import tpu as pltpu
from jax.sharding import PartitionSpec as P

QH = 64
KVH = 8
HD = 128
BLK = 16
GROUP_HEADS = QH // KVH

NEGATIVE = -1e30
EPSILON = 1e-06
LANES = 128
TOKEN_LOG2 = math.log2(math.e) * HD ** (-0.5)
MESH = pl.DeviceIdType.MESH


def kernel(
    nz,
    nt,
    seq_rep,
    local_heads,
    lengths_ref,
    counts_ref,
    slot_seq_hbm,
    slot_block_hbm,
    residual_hbm,
    queries_hbm,
    new_kv_hbm,
    gain_hbm,
    cache_ref,
    weight_ref,
    stream_ref,
    factor_ref,
    slot_seq_ref,
    slot_block_ref,
    residual_ref,
    queries_ref,
    new_kv_ref,
    gain_ref,
    cache_buf,
    weight_buf,
    bias_buf,
    row_buf,
    new_buf,
    q_all,
    part_tp,
    stat_tp,
    part_send,
    stat_send,
    z_send,
    z_stat_send,
    z_part,
    z_stat,
    lhs_buf,
    proj_sum,
    proj_send,
    proj_recv,
    ss_send,
    ss_recv,
    input_sem,
    cache_sem,
    weight_sem,
    qz_send,
    qz_recv,
    qt_send,
    qt_recv,
    pt_send,
    pt_recv,
    st_send,
    st_recv,
    zp_send,
    zp_recv,
    zs_send,
    zs_recv,
    rs_send,
    rs_recv,
    sq_send,
    sq_recv,
):
    z = lax.axis_index("kvb")
    t = lax.axis_index("tp")
    kv_local = max(1, local_heads // GROUP_HEADS)
    per_kv = local_heads // kv_local
    sub = per_kv * seq_rep
    rows = nz * sub
    tokens = cache_buf.shape[0]
    slots = slot_seq_ref.shape[1]
    width = stream_ref.shape[1]
    fast = 2 if nt % 2 == 0 else 1
    slow = nt // fast

    def tp_to(j):
        return lax.rem(t // fast + j // fast, slow) * fast + lax.rem(t % fast + j % fast, fast)

    def tp_from(j):
        back = (slow - j // fast) % slow
        back_fast = (fast - j % fast) % fast
        return lax.rem(t // fast + back, slow) * fast + lax.rem(t % fast + back_fast, fast)

    def z_to(a):
        return lax.rem(z + a, nz)

    def z_back(a):
        return lax.rem(z + (nz - a), nz)

    far_first = sorted(range(1, nt), key=lambda j: (j < fast, j))

    barrier = pltpu.get_barrier_semaphore()
    for a in range(1, nz):
        pl.semaphore_signal(barrier, inc=1, device_id={"kvb": z_to(a)}, device_id_type=MESH)
    for j in range(1, nt):
        pl.semaphore_signal(barrier, inc=1, device_id={"tp": tp_to(j)}, device_id_type=MESH)

    own = pl.ds(pl.multiple_of(t * width, LANES), width)
    inputs = [
        pltpu.make_async_copy(src, dst, input_sem.at[i])
        for i, (src, dst) in enumerate(
            (
                (queries_hbm, queries_ref),
                (slot_seq_hbm, slot_seq_ref),
                (slot_block_hbm, slot_block_ref),
                (new_kv_hbm, new_kv_ref),
                (residual_hbm.at[:, own], residual_ref),
                (gain_hbm, gain_ref),
            )
        )
    ]
    for copy in inputs:
        copy.start()
    cache_copy = pltpu.make_async_copy(cache_ref, cache_buf, cache_sem)
    cache_copy.start()
    inputs[0].wait()

    wide_q = queries_ref[...].astype(jnp.float32)
    for k in range(kv_local):
        for q in range(per_kv):
            head = k * per_kv + q
            row_buf[k, q * seq_rep : (q + 1) * seq_rep, :] = wide_q[:, head * HD : (head + 1) * HD]
    for k in range(kv_local):
        q_all[0, 0, k] = row_buf[k].astype(jnp.bfloat16)
    with jax.named_scope("barrier_wait"):
        pl.semaphore_wait(barrier, nz - 1 + nt - 1)

    pending = []

    def remote(src, dst, send, recv, target):
        copy = pltpu.make_async_remote_copy(
            src_ref=src,
            dst_ref=dst,
            send_sem=send,
            recv_sem=recv,
            device_id=target,
            device_id_type=MESH,
        )
        copy.start()
        pending.append(copy)
        return copy

    z_order = sorted(range(1, nz), key=lambda a: min(a, nz - a))
    q_from_z = {}
    for a in reversed(z_order):
        q_from_z[a] = remote(
            q_all.at[0, 0], q_all.at[0, a], qz_send.at[a], qz_recv.at[a], {"kvb": z_to(a)}
        )
    q_from_tp = {}

    def relayed(j):
        return fast == 2 and j > 2 and j % 2 == 1

    def relay(j):
        for a in [0] + z_order:
            with jax.named_scope(f"q_relay_wait{j}"):
                q_from_tp[a, j].wait_recv()
            q_from_tp[a, j + 1] = remote(
                q_all.at[j, a],
                q_all.at[j + 1, a],
                qt_send.at[a, j + 1],
                qt_recv.at[a, j + 1],
                {"tp": tp_to(1)},
            )

    def forward(a):
        for j in far_first:
            if relayed(j):
                continue
            q_from_tp[a, j] = remote(
                q_all.at[0, a],
                q_all.at[j, a],
                qt_send.at[a, j],
                qt_recv.at[a, j],
                {"tp": tp_to(j)},
            )

    forward(0)

    depth = weight_buf.shape[0] // kv_local
    pieces = 4
    weight_copies = []
    for i in range(kv_local * pieces):
        part_rows = pl.ds(i * (depth // pieces), depth // pieces)
        weight_copies.append(
            pltpu.make_async_copy(
                weight_ref.at[part_rows, :], weight_buf.at[part_rows, :], weight_sem.at[i]
            )
        )
        weight_copies[i].start()
    for copy in inputs[1:]:
        copy.wait()

    row_id = lax.broadcasted_iota(jnp.int32, (rows, slots), 0)
    slot_id = lax.broadcasted_iota(jnp.int32, (rows, slots), 1)
    row_seq = lax.rem(z + nz - row_id // sub, nz) * seq_rep + lax.rem(row_id, seq_rep)
    row_len = jnp.zeros((rows, slots), jnp.int32)
    for s in range(nz * seq_rep):
        row_len = jnp.where(row_seq == s, lengths_ref[s], row_len)
    held = (row_seq == slot_seq_ref[...]) & (slot_id < counts_ref[0])
    limit = jnp.where(held, jnp.clip(row_len - BLK * slot_block_ref[...], 0, BLK), 0)
    token_slot = lax.broadcasted_iota(jnp.int32, (slots, tokens), 1) // BLK
    spread = (token_slot == lax.broadcasted_iota(jnp.int32, (slots, tokens), 0)).astype(jnp.float32)
    reach = jnp.dot(
        limit.astype(jnp.float32).astype(jnp.bfloat16),
        spread.astype(jnp.bfloat16),
        preferred_element_type=jnp.float32,
    )
    offset = lax.rem(lax.broadcasted_iota(jnp.int32, (rows, tokens), 1), BLK).astype(jnp.float32)
    bias_buf[...] = jnp.where(offset < reach, 0.0, NEGATIVE)

    own_kv = t * local_heads // GROUP_HEADS
    fresh = []
    for k in range(kv_local):
        for part in range(2):
            at = pl.multiple_of((part * KVH + own_kv + k) * HD, LANES)
            piece = new_kv_ref[:, pl.ds(at, HD)].astype(jnp.float32)
            for q in range(per_kv):
                new_buf[k, part, q * seq_rep : (q + 1) * seq_rep, :] = piece
        fresh.append(jnp.sum(row_buf[k] * new_buf[k, 0], axis=1, keepdims=True) * TOKEN_LOG2)
    lhs_buf[...] = jnp.zeros_like(lhs_buf)

    for a in z_order:
        with jax.named_scope(f"q_z_wait{a}"):
            q_from_z[a].wait_recv()
        forward(a)

    with jax.named_scope("cache_wait"):
        cache_copy.wait()
    lane = lax.broadcasted_iota(jnp.int32, (rows, LANES), 1)
    copies = {}

    def attend(j, k):
        first_kv = tp_from(j) * local_heads // GROUP_HEADS
        key_at = pl.multiple_of((first_kv + k) * HD, LANES)
        value_at = pl.multiple_of((KVH + first_kv + k) * HD, LANES)
        q_rows = q_all[j, :, k].reshape(rows, HD)
        scores = lax.dot_general(
            q_rows,
            cache_buf[:, pl.ds(key_at, HD)],
            (((1,), (1,)), ((), ())),
            preferred_element_type=jnp.float32,
        )
        scores = scores * TOKEN_LOG2 + bias_buf[...]
        peak = jnp.max(scores, axis=1, keepdims=True)
        weights = jnp.exp2(scores - jnp.maximum(peak, 0.1 * NEGATIVE))
        total = jnp.sum(weights, axis=1, keepdims=True)
        partial = jnp.dot(
            weights.astype(jnp.bfloat16),
            cache_buf[:, pl.ds(value_at, HD)],
            preferred_element_type=jnp.float32,
        ).astype(jnp.bfloat16)
        tile = jnp.where(lane == 0, peak, total).T[:8]
        if j == 0:
            part_tp[0, k] = partial
            stat_tp[0, k] = tile
            return
        part_send[j, k] = partial
        stat_send[j, k] = tile
        target = {"tp": tp_from(j)}
        copies[j, k] = (
            remote(
                stat_send.at[j, k],
                stat_tp.at[j, k],
                st_send.at[j, k],
                st_recv.at[j, k],
                target,
            ),
            remote(
                part_send.at[j, k],
                part_tp.at[j, k],
                pt_send.at[j, k],
                pt_recv.at[j, k],
                target,
            ),
        )

    for k in range(kv_local):
        attend(0, k)
    arrived = set()
    for k in range(kv_local):
        for j in far_first if k == kv_local - 1 else range(1, nt):
            if j not in arrived and relayed(j + 1):
                arrived.add(j)
                relay(j)
            elif j not in arrived:
                arrived.add(j)
                with jax.named_scope(f"q_tp_wait{j}"):
                    for a in range(nz):
                        q_from_tp[a, j].wait_recv()
            attend(j, k)

    def columns_of(pieces):
        height = -(-len(pieces) // 8) * 8
        index = lax.broadcasted_iota(jnp.int32, (height, rows), 0)
        tile = jnp.zeros((height, rows), jnp.float32)
        for i, piece in enumerate(pieces):
            tile = jnp.where(index == i, piece, tile)
        return tile.T

    from_z = {}
    for k in range(kv_local):
        with jax.named_scope(f"part_wait{k}"):
            for j in range(1, nt):
                for copy in copies[j, k]:
                    copy.wait_recv()
        peaks = [stat_tp[j, k, 0:1, :] for j in range(nt)]
        top = peaks[0]
        for piece in peaks[1:]:
            top = jnp.maximum(top, piece)
        scale = [jnp.exp2(piece - top) for piece in peaks]
        total = scale[0] * stat_tp[0, k, 1:2, :]
        for j in range(1, nt):
            total += scale[j] * stat_tp[j, k, 1:2, :]
        spread_scale = columns_of(scale)
        joined = spread_scale[:, 0:1] * part_tp[0, k].astype(jnp.float32)
        for j in range(1, nt):
            joined += spread_scale[:, j : j + 1] * part_tp[j, k].astype(jnp.float32)
        joined = joined.astype(jnp.bfloat16)
        index = lax.broadcasted_iota(jnp.int32, (8, rows), 0)
        tile = jnp.where(index == 0, top, total)
        z_stat_send[k] = tile
        z_stat[0, k] = tile
        z_part[0, k] = joined[:sub]
        for a in range(1, nz):
            z_send[a, k] = joined[a * sub : (a + 1) * sub]
        for a in reversed(z_order):
            target = {"kvb": z_back(a)}
            from_z[a, k] = (
                remote(
                    z_stat_send.at[k],
                    z_stat.at[a, k],
                    zs_send.at[a, k],
                    zs_recv.at[a, k],
                    target,
                ),
                remote(
                    z_send.at[a, k],
                    z_part.at[a, k],
                    zp_send.at[a, k],
                    zp_recv.at[a, k],
                    target,
                ),
            )

    step = width
    reduced = {}
    for k in range(kv_local):
        with jax.named_scope(f"z_wait{k}"):
            for a in z_order:
                for copy in from_z[a, k]:
                    copy.wait_recv()
        spread_stat = columns_of([z_stat[a, k, i : i + 1, :] for a in range(nz) for i in range(2)])
        peaks = [spread_stat[a * sub : (a + 1) * sub, 2 * a : 2 * a + 1] for a in range(nz)]
        sums = [spread_stat[a * sub : (a + 1) * sub, 2 * a + 1 : 2 * a + 2] for a in range(nz)]
        top = fresh[k]
        for piece in peaks:
            top = jnp.maximum(top, piece)
        denominator = jnp.exp2(fresh[k] - top)
        numerator = denominator * new_buf[k, 1]
        for a in range(nz):
            scale = jnp.exp2(peaks[a] - top)
            denominator += scale * sums[a]
            numerator += scale * z_part[a, k].astype(jnp.float32)
        row_buf[k] = numerator / denominator
        for q in range(per_kv):
            lhs_buf[k, 0:seq_rep, q * HD : (q + 1) * HD] = row_buf[
                k, q * seq_rep : (q + 1) * seq_rep, :
            ]
        attended = lhs_buf[k].astype(jnp.bfloat16)
        with jax.named_scope(f"weight_wait{k}"):
            for copy in weight_copies[k * pieces : (k + 1) * pieces]:
                copy.wait()
        for j in far_first + [0]:
            column = tp_to(j) * width

            def column_step(i, carry, j=j, k=k, column=column, attended=attended):
                at = pl.ds(pl.multiple_of(i * step, LANES), step)
                source = pl.ds(pl.multiple_of(column + i * step, LANES), step)
                got = jnp.dot(
                    attended,
                    weight_buf[k * depth : (k + 1) * depth, source],
                    preferred_element_type=jnp.float32,
                )[:seq_rep]
                if k > 0:
                    got += proj_sum[j, :, at]
                if j > 0 and k == kv_local - 1:
                    proj_send[j, :, at] = got.astype(jnp.bfloat16)
                else:
                    proj_sum[j, :, at] = got
                return carry

            lax.fori_loop(0, width // step, column_step, 0)
            if j > 0 and k == kv_local - 1:
                reduced[j] = remote(
                    proj_send.at[j],
                    proj_recv.at[j],
                    rs_send.at[j],
                    rs_recv.at[j],
                    {"tp": tp_to(j)},
                )
    summed = proj_sum[0]
    with jax.named_scope("sum_wait"):
        for j in far_first:
            reduced[j].wait_recv()
    for j in far_first:
        summed += proj_recv[j].astype(jnp.float32)
    stream = (residual_ref[...].astype(jnp.float32) + summed).astype(jnp.bfloat16)
    stream_wide = stream.astype(jnp.float32)
    stream_ref[...] = stream_wide
    square = jnp.sum(stream_wide * stream_wide, axis=1, keepdims=True)
    ss_send[...] = jnp.broadcast_to(square, ss_send.shape)
    squares = [
        remote(ss_send, ss_recv.at[j], sq_send.at[j], sq_recv.at[j], {"tp": tp_to(j)})
        for j in far_first
    ]
    gain = gain_ref[...].astype(jnp.float32).reshape(1, width)
    with jax.named_scope("square_wait"):
        for copy in squares:
            copy.wait_recv()
    for j in range(1, nt):
        square += ss_recv[j][:, 0:1]
    mean_square = square * (1.0 / (width * nt))
    factor_ref[...] = lax.rsqrt(mean_square + EPSILON) * gain
    for copy in pending:
        copy.wait_send()


def on_device(
    residual,
    queries,
    new_kv,
    kv_cache,
    lengths,
    slot_seq,
    slot_block,
    block_counts,
    out_weight,
    norm_gain,
):
    nt = lax.axis_size("tp")
    nz = lax.axis_size("kvb")
    seq_rep = residual.shape[0]
    local_heads = queries.shape[1] // HD
    kv_local = max(1, local_heads // GROUP_HEADS)
    sub = local_heads // kv_local * seq_rep
    rows = nz * sub
    slots = kv_cache.shape[0]
    tokens = slots * BLK
    width = norm_gain.shape[0]
    depth = out_weight.shape[0]
    bf16, f32 = jnp.bfloat16, jnp.float32
    dma = pltpu.SemaphoreType.DMA
    vmem = pl.BlockSpec(memory_space=pltpu.VMEM)
    smem = pl.BlockSpec(memory_space=pltpu.SMEM)
    hbm = pl.BlockSpec(memory_space=pl.ANY)

    def body(*refs):
        kernel(nz, nt, seq_rep, local_heads, *refs)

    stream, factor = pl.pallas_call(
        body,
        out_shape=(
            jax.ShapeDtypeStruct((seq_rep, width), f32),
            jax.ShapeDtypeStruct((seq_rep, width), f32),
        ),
        in_specs=[smem, smem] + [hbm] * 8,
        out_specs=(vmem, vmem),
        scratch_shapes=[
            pltpu.VMEM((1, slots), jnp.int32),
            pltpu.VMEM((1, slots), jnp.int32),
            pltpu.VMEM((seq_rep, width), bf16),
            pltpu.VMEM(queries.shape, bf16),
            pltpu.VMEM(new_kv.shape, bf16),
            pltpu.VMEM((width,), bf16),
            pltpu.VMEM((tokens, kv_cache.shape[2]), bf16),
            pltpu.VMEM(out_weight.shape, bf16),
            pltpu.VMEM((rows, tokens), f32),
            pltpu.VMEM((kv_local, sub, HD), f32),
            pltpu.VMEM((kv_local, 2, sub, HD), f32),
            pltpu.VMEM((nt, nz, kv_local, sub, HD), bf16),
            pltpu.VMEM((nt, kv_local, rows, HD), bf16),
            pltpu.VMEM((nt, kv_local, 8, rows), f32),
            pltpu.VMEM((nt, kv_local, rows, HD), bf16),
            pltpu.VMEM((nt, kv_local, 8, rows), f32),
            pltpu.VMEM((nz, kv_local, sub, HD), bf16),
            pltpu.VMEM((kv_local, 8, rows), f32),
            pltpu.VMEM((nz, kv_local, sub, HD), bf16),
            pltpu.VMEM((nz, kv_local, 8, rows), f32),
            pltpu.VMEM((kv_local, 16, depth // kv_local), f32),
            pltpu.VMEM((nt, seq_rep, width), f32),
            pltpu.VMEM((nt, seq_rep, width), bf16),
            pltpu.VMEM((nt, seq_rep, width), bf16),
            pltpu.VMEM((seq_rep, LANES), f32),
            pltpu.VMEM((nt, seq_rep, LANES), f32),
            dma((6,)),
            dma,
            dma((kv_local * 4,)),
            dma((nz,)),
            dma((nz,)),
            dma((nz, nt)),
            dma((nz, nt)),
            dma((nt, kv_local)),
            dma((nt, kv_local)),
            dma((nt, kv_local)),
            dma((nt, kv_local)),
            dma((nz, kv_local)),
            dma((nz, kv_local)),
            dma((nz, kv_local)),
            dma((nz, kv_local)),
            dma((nt,)),
            dma((nt,)),
            dma((nt,)),
            dma((nt,)),
        ],
        compiler_params=pltpu.CompilerParams(
            collective_id=0, has_side_effects=True, vmem_limit_bytes=62 * 1024 * 1024
        ),
    )(
        lengths,
        block_counts,
        slot_seq.reshape(1, slots),
        slot_block.reshape(1, slots),
        residual,
        queries,
        new_kv,
        norm_gain,
        kv_cache.reshape(tokens, kv_cache.shape[2]),
        out_weight,
    )
    return (stream.astype(bf16), (stream * factor).astype(bf16))


def solution(mesh):
    placed = (
        P(("groups", "kvb"), None),
        P(("groups", "kvb"), "tp"),
        P(("groups", "kvb"), None),
        P(("groups", "kvb", "tp"), None, None),
        P("groups"),
        P(("groups", "kvb", "tp")),
        P(("groups", "kvb", "tp")),
        P(("groups", "kvb", "tp")),
        P("tp", None),
        P("tp"),
    )
    return jax.shard_map(
        on_device,
        mesh=mesh,
        in_specs=placed,
        out_specs=(P(("groups", "kvb"), "tp"), P(("groups", "kvb"), "tp")),
        check_vma=False,
    )
```

profile of v0, /device:TPU:0, one launch (start us, length us, event | category | flops | bytes accessed | tf_op | source)
XLA Modules:
  0.0 34.8 jit_solution(3162168703374730989)
XLA Ops:
  1.3 32.0 %shard_map.113 = (f32[4,2048]{1,0:T(4,128)}, f32[4,2048]{1,0:T(4,128)}) custom-call(s32[16]{0:T(128)} %refs_0_.1, s32[1]{0:T(128)S(6)} %copy.12.refs_1_, s32[1,64]{1,0:T(1,128)} %bitcast.4, s32[1,64]{1,0:T(1,128)} %bitcast.5, bf16[4,8192]{1,0:T(4,128)(2,1)} %refs_4_.1, bf16[4,2048]{1,0:T(4,128)(2,1)} %refs_5_.1, bf16[4,2048]{1,0:T(4,128)(2,1)} %refs_6_.1, ...), custom_call_target="tpu_custom_call" | custom-call | tf_op jit(solution)/shard_map/pallas_call | solution.py:483
  33.3 1.5 %multiply_convert_fusion = (bf16[4,2048]{1,0:T(4,128)(2,1)}, bf16[4,2048]{1,0:T(4,128)(2,1)}) fusion(f32[4,2048]{1,0:T(4,128)} %get-tuple-element.4, f32[4,2048]{1,0:T(4,128)} %get-tuple-element.5), kind=kLoop, calls=%fused_computation | loop fusion | flops 24576 | bytes 98304 | tf_op jit(solution)/shard_map/convert_element_type | solution.py:553
where the time goes:
time: 35 us; the launch traced here: 34.8 us
  Pallas kernels  32 us (91%)
  other arithmetic  1.46 us (4%)
  between operations  1.29 us (4%)
    pallas_call x1, Pallas kernels, on_device(): pl.pallas_call(body, out_shape=(jax.ShapeDtypeStruct((seq_rep, width), f3...  32 us
    convert_element_type x1, other arithmetic, on_device(): return (stream.astype(bf16), (stream * factor).astype(bf16))  1.46 us

commit v1 on v0

--- a/solution.py
+++ b/solution.py
@@ -25,8 +25,8 @@
     nt,
     seq_rep,
     local_heads,
-    lengths_ref,
     counts_ref,
+    lengths_hbm,
     slot_seq_hbm,
     slot_block_hbm,
     residual_hbm,
@@ -37,12 +37,14 @@
     weight_ref,
     stream_ref,
     factor_ref,
+    lengths_ref,
     slot_seq_ref,
     slot_block_ref,
     residual_ref,
     queries_ref,
     new_kv_ref,
     gain_ref,
+    wide_gain,
     cache_buf,
     weight_buf,
     bias_buf,
@@ -128,6 +130,7 @@
                 (new_kv_hbm, new_kv_ref),
                 (residual_hbm.at[:, own], residual_ref),
                 (gain_hbm, gain_ref),
+                (lengths_hbm, lengths_ref),
             )
         )
     ]
@@ -241,6 +244,8 @@
                 new_buf[k, part, q * seq_rep : (q + 1) * seq_rep, :] = piece
         fresh.append(jnp.sum(row_buf[k] * new_buf[k, 0], axis=1, keepdims=True) * TOKEN_LOG2)
     lhs_buf[...] = jnp.zeros_like(lhs_buf)
+    gain = gain_ref[...].astype(jnp.float32).reshape(1, width)
+    wide_gain[...] = jnp.broadcast_to(gain, wide_gain.shape)
 
     for a in z_order:
         with jax.named_scope(f"q_z_wait{a}"):
@@ -421,13 +426,16 @@
                     rs_recv.at[j],
                     {"tp": tp_to(j)},
                 )
-    summed = proj_sum[0]
+    summed = residual_ref[...].astype(jnp.float32) + proj_sum[0]
+    for copy in pending[: -len(reduced)]:
+        copy.wait_send()
+    del pending[: -len(reduced)]
     with jax.named_scope("sum_wait"):
         for j in far_first:
             reduced[j].wait_recv()
     for j in far_first:
         summed += proj_recv[j].astype(jnp.float32)
-    stream = (residual_ref[...].astype(jnp.float32) + summed).astype(jnp.bfloat16)
+    stream = summed.astype(jnp.bfloat16)
     stream_wide = stream.astype(jnp.float32)
     stream_ref[...] = stream_wide
     square = jnp.sum(stream_wide * stream_wide, axis=1, keepdims=True)
@@ -436,14 +444,13 @@
         remote(ss_send, ss_recv.at[j], sq_send.at[j], sq_recv.at[j], {"tp": tp_to(j)})
         for j in far_first
     ]
-    gain = gain_ref[...].astype(jnp.float32).reshape(1, width)
     with jax.named_scope("square_wait"):
         for copy in squares:
             copy.wait_recv()
     for j in range(1, nt):
         square += ss_recv[j][:, 0:1]
     mean_square = square * (1.0 / (width * nt))
-    factor_ref[...] = lax.rsqrt(mean_square + EPSILON) * gain
+    factor_ref[...] = lax.rsqrt(mean_square + EPSILON) * wide_gain[...]
     for copy in pending:
         copy.wait_send()
 
@@ -473,8 +480,8 @@
     depth = out_weight.shape[0]
     bf16, f32 = jnp.bfloat16, jnp.float32
     dma = pltpu.SemaphoreType.DMA
+    smem = pl.BlockSpec(memory_space=pltpu.SMEM)
     vmem = pl.BlockSpec(memory_space=pltpu.VMEM)
-    smem = pl.BlockSpec(memory_space=pltpu.SMEM)
     hbm = pl.BlockSpec(memory_space=pl.ANY)
 
     def body(*refs):
@@ -486,15 +493,17 @@
             jax.ShapeDtypeStruct((seq_rep, width), f32),
             jax.ShapeDtypeStruct((seq_rep, width), f32),
         ),
-        in_specs=[smem, smem] + [hbm] * 8,
+        in_specs=[smem] + [hbm] * 9,
         out_specs=(vmem, vmem),
         scratch_shapes=[
+            pltpu.SMEM(lengths.shape, jnp.int32),
             pltpu.VMEM((1, slots), jnp.int32),
             pltpu.VMEM((1, slots), jnp.int32),
             pltpu.VMEM((seq_rep, width), bf16),
             pltpu.VMEM(queries.shape, bf16),
             pltpu.VMEM(new_kv.shape, bf16),
             pltpu.VMEM((width,), bf16),
+            pltpu.VMEM((seq_rep, width), f32),
             pltpu.VMEM((tokens, kv_cache.shape[2]), bf16),
             pltpu.VMEM(out_weight.shape, bf16),
             pltpu.VMEM((rows, tokens), f32),
@@ -515,7 +524,7 @@
             pltpu.VMEM((nt, seq_rep, width), bf16),
             pltpu.VMEM((seq_rep, LANES), f32),
             pltpu.VMEM((nt, seq_rep, LANES), f32),
-            dma((6,)),
+            dma((7,)),
             dma,
             dma((kv_local * 4,)),
             dma((nz,)),
@@ -536,19 +545,24 @@
             dma((nt,)),
         ],
         compiler_params=pltpu.CompilerParams(
-            collective_id=0, has_side_effects=True, vmem_limit_bytes=62 * 1024 * 1024
+            collective_id=0, has_side_effects=True, vmem_limit_bytes=46 * 1024 * 1024
         ),
     )(
-        lengths,
         block_counts,
-        slot_seq.reshape(1, slots),
-        slot_block.reshape(1, slots),
-        residual,
-        queries,
-        new_kv,
-        norm_gain,
-        kv_cache.reshape(tokens, kv_cache.shape[2]),
-        out_weight,
+        *(
+            pltpu.with_memory_space_constraint(operand, pltpu.HBM)
+            for operand in (
+                lengths,
+                slot_seq.reshape(1, slots),
+                slot_block.reshape(1, slots),
+                residual,
+                queries,
+                new_kv,
+                norm_gain,
+                kv_cache.reshape(tokens, kv_cache.shape[2]),
+                out_weight,
+            )
+        )
     )
     return (stream.astype(bf16), (stream * factor).astype(bf16))
 

time: 35 us -> 32.8 us (0.937)
  Pallas kernels: 32 us -> 30.7 us
  other arithmetic: 1.46 us -> 0.63 us
    pallas_call x1, Pallas kernels: 32 us -> 30.7 us  [on_device(): pl.pallas_call(body, out_shape=(jax.ShapeDtypeStruct((seq_rep, width), f3...]
    convert_element_type x1, other arithmetic: 1.46 us -> 0.63 us  [on_device(): return (stream.astype(bf16), (stream * factor).astype(bf16))]
where the time goes in v1:
time: 32.8 us; the launch traced here: 32.6 us
  Pallas kernels  30.7 us (94%)
  between operations  1.29 us (4%)
  other arithmetic  0.63 us (2%)
    pallas_call x1, Pallas kernels, on_device(): pl.pallas_call(body, out_shape=(jax.ShapeDtypeStruct((seq_rep, width), f3...  30.7 us

profile of v1, /device:TPU:0, one launch (start us, length us, event | category | flops | bytes accessed | tf_op | source)
XLA Modules:
  0.0 32.6 jit_solution(6507989106526534761)
XLA Ops:
  1.3 30.7 %shard_map.113 = (f32[4,2048]{1,0:T(4,128)S(1)}, f32[4,2048]{1,0:T(4,128)S(1)}) custom-call(s32[1]{0:T(128)S(6)} %copy.12.refs_0_, s32[16]{0:T(128)} %refs_1_.1, s32[1,64]{1,0:T(1,128)} %bitcast.4, s32[1,64]{1,0:T(1,128)} %bitcast.5, bf16[4,8192]{1,0:T(4,128)(2,1)} %refs_4_.1, bf16[4,2048]{1,0:T(4,128)(2,1)} %refs_5_.1, bf16[4,2048]{1,0:T(4,128)(2,1)} %refs_6_.1, ...), custom_call_target="tpu_custom_call" | custom-call | tf_op jit(solution)/shard_map/pallas_call | solution.py:490
  32.0 0.6 %multiply_convert_fusion = (bf16[4,2048]{1,0:T(4,128)(2,1)}, bf16[4,2048]{1,0:T(4,128)(2,1)}) fusion(f32[4,2048]{1,0:T(4,128)S(1)} %get-tuple-element.4, f32[4,2048]{1,0:T(4,128)S(1)} %get-tuple-element.5), kind=kLoop, calls=%fused_computation | loop fusion | flops 24576 | bytes 98304 | tf_op jit(solution)/shard_map/convert_element_type | solution.py:567

commit v2 on v1

v2 whole, which is shorter than its diff:
```python
import math

import jax
import jax.numpy as jnp
from jax import lax
from jax.experimental import pallas as pl
from jax.experimental.pallas import tpu as pltpu
from jax.sharding import PartitionSpec as P

QH = 64
KVH = 8
HD = 128
BLK = 16
GROUP_HEADS = QH // KVH

NEGATIVE = -1e30
EPSILON = 1e-06
LANES = 128
CORES = 2
TOKEN_LOG2 = math.log2(math.e) * HD ** (-0.5)
MESH = pl.DeviceIdType.MESH


def flipped(index, mask):
    out = index
    bit = 1
    while bit <= mask:
        if mask & bit:
            out = out + bit * (1 - 2 * lax.rem(index // bit, 2))
        bit *= 2
    return out


def kernel(
    nz,
    nt,
    seq_rep,
    local_heads,
    counts_ref,
    lengths_hbm,
    slot_seq_hbm,
    slot_block_hbm,
    residual_hbm,
    queries_hbm,
    new_kv_hbm,
    gain_hbm,
    cache_ref,
    weight_ref,
    stream_ref,
    factor_ref,
    lengths_ref,
    slot_seq_ref,
    slot_block_ref,
    residual_ref,
    queries_ref,
    new_kv_ref,
    gain_ref,
    wide_gain,
    cache_buf,
    weight_buf,
    bias_buf,
    row_buf,
    new_buf,
    q_all,
    pair_send,
    pair_recv,
    z_send,
    z_stat_send,
    z_part,
    z_stat,
    lhs_buf,
    proj_sum,
    proj_send,
    proj_recv,
    ss_send,
    ss_recv,
    input_sem,
    cache_sem,
    weight_sem,
    qz_recv,
    qt_recv,
    pair_sem,
    zp_recv,
    zs_recv,
    send_sem,
    rs_recv,
    sq_recv,
):
    z = lax.axis_index("kvb")
    t = lax.axis_index("tp")
    kv_local = max(1, local_heads // GROUP_HEADS)
    per_kv = local_heads // kv_local
    sub = per_kv * seq_rep
    rows = nz * sub
    tokens = cache_buf.shape[0]
    slots = slot_seq_ref.shape[1]
    width = stream_ref.shape[1]
    slow = nt // CORES
    QZ, QT, PAIR, ZP, ZS, RS, SQ = range(7)

    def z_peer(a):
        return flipped(z, a)

    def tp_peer(j):
        return flipped(t, j)

    far_first = sorted(range(1, nt), key=lambda j: (j < CORES, j))

    barrier = pltpu.get_barrier_semaphore()
    for a in range(1, nz):
        pl.semaphore_signal(barrier, inc=1, device_id={"kvb": z_peer(a)}, device_id_type=MESH)
    for j in range(1, nt):
        pl.semaphore_signal(barrier, inc=1, device_id={"tp": tp_peer(j)}, device_id_type=MESH)

    own = pl.ds(pl.multiple_of(t * width, LANES), width)
    inputs = [
        pltpu.make_async_copy(src, dst, input_sem.at[i])
        for i, (src, dst) in enumerate(
            (
                (queries_hbm, queries_ref),
                (slot_seq_hbm, slot_seq_ref),
                (slot_block_hbm, slot_block_ref),
                (new_kv_hbm, new_kv_ref),
                (residual_hbm.at[:, own], residual_ref),
                (gain_hbm, gain_ref),
                (lengths_hbm, lengths_ref),
            )
        )
    ]
    for copy in inputs:
        copy.start()
    cache_copy = pltpu.make_async_copy(cache_ref, cache_buf, cache_sem)
    cache_copy.start()
    inputs[0].wait()

    wide_q = queries_ref[...].astype(jnp.float32)
    for k in range(kv_local):
        for q in range(per_kv):
            head = k * per_kv + q
            row_buf[k, q * seq_rep : (q + 1) * seq_rep, :] = wide_q[:, head * HD : (head + 1) * HD]
    for k in range(kv_local):
        q_all[0, 0, k] = row_buf[k].astype(jnp.bfloat16)
    with jax.named_scope("barrier_wait"):
        pl.semaphore_wait(barrier, nz - 1 + nt - 1)

    def remote(src, dst, send, recv, target):
        pltpu.make_async_remote_copy(
            src_ref=src,
            dst_ref=dst,
            send_sem=send_sem.at[send],
            recv_sem=recv,
            device_id=target,
            device_id_type=MESH,
        ).start()

    def wait_bytes(ref, sem):
        pltpu.make_async_copy(ref, ref, sem).wait()

    for a in reversed(range(1, nz)):
        remote(q_all.at[0, 0], q_all.at[0, a], QZ, qz_recv.at[a - 1], {"kvb": z_peer(a)})

    def forward(a):
        for j in far_first:
            remote(q_all.at[0, a], q_all.at[j, a], QT, qt_recv.at[j - 1], {"tp": tp_peer(j)})

    forward(0)

    depth = weight_buf.shape[0] // kv_local
    pieces = 4
    for i in range(kv_local * pieces):
        part_rows = pl.ds(i * (depth // pieces), depth // pieces)
        pltpu.make_async_copy(
            weight_ref.at[part_rows, :], weight_buf.at[part_rows, :], weight_sem.at[i // pieces]
        ).start()
    for copy in inputs[1:]:
        copy.wait()

    row_id = lax.broadcasted_iota(jnp.int32, (rows, slots), 0)
    slot_id = lax.broadcasted_iota(jnp.int32, (rows, slots), 1)
    row_seq = jnp.zeros((rows, slots), jnp.int32)
    for a in range(nz):
        row_seq = jnp.where(row_id // sub == a, z_peer(a) * seq_rep, row_seq)
    row_seq += lax.rem(row_id, seq_rep)
    row_len = jnp.zeros((rows, slots), jnp.int32)
    for s in range(nz * seq_rep):
        row_len = jnp.where(row_seq == s, lengths_ref[s], row_len)
    held = (row_seq == slot_seq_ref[...]) & (slot_id < counts_ref[0])
    limit = jnp.where(held, jnp.clip(row_len - BLK * slot_block_ref[...], 0, BLK), 0)
    token_slot = lax.broadcasted_iota(jnp.int32, (slots, tokens), 1) // BLK
    spread = (token_slot == lax.broadcasted_iota(jnp.int32, (slots, tokens), 0)).astype(jnp.float32)
    reach = jnp.dot(
        limit.astype(jnp.float32).astype(jnp.bfloat16),
        spread.astype(jnp.bfloat16),
        preferred_element_type=jnp.float32,
    )
    offset = lax.rem(lax.broadcasted_iota(jnp.int32, (rows, tokens), 1), BLK).astype(jnp.float32)
    bias_buf[...] = jnp.where(offset < reach, 0.0, NEGATIVE)

    own_kv = t * local_heads // GROUP_HEADS
    fresh = []
    for k in range(kv_local):
        for part in range(2):
            at = pl.multiple_of((part * KVH + own_kv + k) * HD, LANES)
            piece = new_kv_ref[:, pl.ds(at, HD)].astype(jnp.float32)
            for q in range(per_kv):
                new_buf[k, part, q * seq_rep : (q + 1) * seq_rep, :] = piece
        fresh.append(jnp.sum(row_buf[k] * new_buf[k, 0], axis=1, keepdims=True) * TOKEN_LOG2)
    lhs_buf[...] = jnp.zeros_like(lhs_buf)
    gain = gain_ref[...].astype(jnp.float32).reshape(1, width)
    wide_gain[...] = jnp.broadcast_to(gain, wide_gain.shape)

    for a in range(1, nz):
        with jax.named_scope(f"q_z_wait{a}"):
            wait_bytes(q_all.at[0, a], qz_recv.at[a - 1])
        forward(a)

    with jax.named_scope("cache_wait"):
        cache_copy.wait()
    lane = lax.broadcasted_iota(jnp.int32, (rows, LANES), 1)
    kept = {}

    def attend(j, k):
        first_kv = tp_peer(j) * local_heads // GROUP_HEADS
        key_at = pl.multiple_of((first_kv + k) * HD, LANES)
        value_at = pl.multiple_of((KVH + first_kv + k) * HD, LANES)
        q_rows = q_all[j, :, k].reshape(rows, HD)
        scores = lax.dot_general(
            q_rows,
            cache_buf[:, pl.ds(key_at, HD)],
            (((1,), (1,)), ((), ())),
            preferred_element_type=jnp.float32,
        )
        scores = scores * TOKEN_LOG2 + bias_buf[...]
        peak = jnp.max(scores, axis=1, keepdims=True)
        weights = jnp.exp2(scores - jnp.maximum(peak, 0.1 * NEGATIVE))
        total = jnp.sum(weights, axis=1, keepdims=True)
        partial = jnp.dot(
            weights.astype(jnp.bfloat16),
            cache_buf[:, pl.ds(value_at, HD)],
            preferred_element_type=jnp.float32,
        )
        wide_peak = jnp.broadcast_to(peak, (rows, HD))
        wide_total = jnp.broadcast_to(total, (rows, HD))
        if j % CORES:
            kept[j // CORES, k] = (partial, wide_peak, wide_total)
            return
        for i, piece in enumerate((partial, wide_peak, wide_total)):
            pair_send[j // CORES, k, i] = piece
        remote(
            pair_send.at[j // CORES, k],
            pair_recv.at[j // CORES, k],
            PAIR,
            pair_sem.at[j // CORES * kv_local + k],
            {"tp": tp_peer(1)},
        )

    def join(jx, k):
        with jax.named_scope(f"pair_wait{jx}{k}"):
            wait_bytes(pair_recv.at[jx, k], pair_sem.at[jx * kv_local + k])
        partial, peak, total = kept.pop((jx, k))
        other, other_peak, other_total = (pair_recv[jx, k, i] for i in range(3))
        top = jnp.maximum(peak, other_peak)
        scale = jnp.exp2(peak - top)
        other_scale = jnp.exp2(other_peak - top)
        joined = scale * partial + other_scale * other
        z_send[jx, k] = joined.astype(jnp.bfloat16)
        total = scale * total + other_scale * other_total
        z_stat_send[jx, k] = jnp.where(lane == 0, top, total).T[:2]
        for a in reversed(range(nz)):
            target = {"kvb": z_peer(a), "tp": tp_peer(jx * CORES + 1)}
            remote(z_stat_send.at[jx, k], z_stat.at[k, jx, a], ZS, zs_recv.at[k], target)
            remote(
                z_send.at[jx, k, pl.ds(a * sub, sub)],
                z_part.at[k, jx, a],
                ZP,
                zp_recv.at[k],
                target,
            )

    for jx in range(slow):
        for jc in range(CORES):
            j = jx * CORES + jc
            if j > 0:
                with jax.named_scope(f"q_tp_wait{j}"):
                    wait_bytes(q_all.at[j], qt_recv.at[j - 1])
            for k in range(kv_local):
                attend(j, k)
                if jc and jx:
                    join(jx, k)
        if jx == 0:
            for k in range(kv_local):
                join(jx, k)

    def columns_of(pieces):
        height = -(-len(pieces) // 8) * 8
        index = lax.broadcasted_iota(jnp.int32, (height, rows), 0)
        tile = jnp.zeros((height, rows), jnp.float32)
        for i, piece in enumerate(pieces):
            tile = jnp.where(index == i, piece, tile)
        return tile.T

    sources = [(jx, a) for jx in range(slow) for a in range(nz)]
    for k in range(kv_local):
        with jax.named_scope(f"z_wait{k}"):
            wait_bytes(z_part.at[k], zp_recv.at[k])
            wait_bytes(z_stat.at[k], zs_recv.at[k])
        spread_stat = columns_of([z_stat[k, jx, a, i : i + 1, :] for jx, a in sources for i in range(2)])
        peaks, sums = (
            [
                spread_stat[a * sub : (a + 1) * sub, 2 * n + i : 2 * n + i + 1]
                for n, (_, a) in enumerate(sources)
            ]
            for i in range(2)
        )
        top = fresh[k]
        for piece in peaks:
            top = jnp.maximum(top, piece)
        denominator = jnp.exp2(fresh[k] - top)
        numerator = denominator * new_buf[k, 1]
        for n, (jx, a) in enumerate(sources):
            scale = jnp.exp2(peaks[n] - top)
            denominator += scale * sums[n]
            numerator += scale * z_part[k, jx, a].astype(jnp.float32)
        row_buf[k] = numerator / denominator
        for q in range(per_kv):
            lhs_buf[k, 0:seq_rep, q * HD : (q + 1) * HD] = row_buf[
                k, q * seq_rep : (q + 1) * seq_rep, :
            ]
        attended = lhs_buf[k].astype(jnp.bfloat16)
        with jax.named_scope(f"weight_wait{k}"):
            half = pl.ds(k * depth, depth)
            pltpu.make_async_copy(
                weight_ref.at[half, :], weight_buf.at[half, :], weight_sem.at[k]
            ).wait()
        for j in far_first + [0]:
            column = pl.ds(pl.multiple_of(tp_peer(j) * width, LANES), width)
            got = jnp.dot(
                attended,
                weight_buf[k * depth : (k + 1) * depth, column],
                preferred_element_type=jnp.float32,
            )[:seq_rep]
            if k > 0:
                got += proj_sum[j]
            if j == 0 or k < kv_local - 1:
                proj_sum[j] = got
                continue
            proj_send[j - 1] = got.astype(jnp.bfloat16)
            remote(proj_send.at[j - 1], proj_recv.at[j - 1], RS, rs_recv, {"tp": tp_peer(j)})
    summed = residual_ref[...].astype(jnp.float32) + proj_sum[0]
    for ref, send in (
        (q_all.at[0, pl.ds(1, nz - 1)], QZ),
        (q_all.at[pl.ds(1, nt - 1)], QT),
        (pair_send, PAIR),
        (z_part, ZP),
        (z_stat, ZS),
    ):
        wait_bytes(ref, send_sem.at[send])
    with jax.named_scope("sum_wait"):
        wait_bytes(proj_recv, rs_recv)
    for j in range(1, nt):
        summed += proj_recv[j - 1].astype(jnp.float32)
    stream = summed.astype(jnp.bfloat16)
    stream_wide = stream.astype(jnp.float32)
    stream_ref[...] = stream_wide
    square = jnp.sum(stream_wide * stream_wide, axis=1, keepdims=True)
    ss_send[...] = jnp.broadcast_to(square, ss_send.shape)
    for j in far_first:
        remote(ss_send, ss_recv.at[j - 1], SQ, sq_recv, {"tp": tp_peer(j)})
    with jax.named_scope("square_wait"):
        wait_bytes(ss_recv, sq_recv)
    for j in range(1, nt):
        square += ss_recv[j - 1][:, 0:1]
    mean_square = square * (1.0 / (width * nt))
    factor_ref[...] = lax.rsqrt(mean_square + EPSILON) * wide_gain[...]
    wait_bytes(proj_send, send_sem.at[RS])
    wait_bytes(ss_recv, send_sem.at[SQ])


def on_device(
    residual,
    queries,
    new_kv,
    kv_cache,
    lengths,
    slot_seq,
    slot_block,
    block_counts,
    out_weight,
    norm_gain,
):
    nt = lax.axis_size("tp")
    nz = lax.axis_size("kvb")
    seq_rep = residual.shape[0]
    local_heads = queries.shape[1] // HD
    kv_local = max(1, local_heads // GROUP_HEADS)
    sub = local_heads // kv_local * seq_rep
    rows = nz * sub
    slots = kv_cache.shape[0]
    tokens = slots * BLK
    width = norm_gain.shape[0]
    depth = out_weight.shape[0]
    slow = nt // CORES
    bf16, f32 = jnp.bfloat16, jnp.float32
    dma = pltpu.SemaphoreType.DMA
    smem = pl.BlockSpec(memory_space=pltpu.SMEM)
    vmem = pl.BlockSpec(memory_space=pltpu.VMEM)
    hbm = pl.BlockSpec(memory_space=pltpu.HBM)

    def body(*refs):
        kernel(nz, nt, seq_rep, local_heads, *refs)

    stream, factor = pl.pallas_call(
        body,
        out_shape=(
            jax.ShapeDtypeStruct((seq_rep, width), f32),
            jax.ShapeDtypeStruct((seq_rep, width), f32),
        ),
        in_specs=[smem] + [hbm] * 9,
        out_specs=(vmem, vmem),
        scratch_shapes=[
            pltpu.SMEM(lengths.shape, jnp.int32),
            pltpu.VMEM((1, slots), jnp.int32),
            pltpu.VMEM((1, slots), jnp.int32),
            pltpu.VMEM((seq_rep, width), bf16),
            pltpu.VMEM(queries.shape, bf16),
            pltpu.VMEM(new_kv.shape, bf16),
            pltpu.VMEM((width,), bf16),
            pltpu.VMEM((seq_rep, width), f32),
            pltpu.VMEM((tokens, kv_cache.shape[2]), bf16),
            pltpu.VMEM(out_weight.shape, bf16),
            pltpu.VMEM((rows, tokens), f32),
            pltpu.VMEM((kv_local, sub, HD), f32),
            pltpu.VMEM((kv_local, 2, sub, HD), f32),
            pltpu.VMEM((nt, nz, kv_local, sub, HD), bf16),
            pltpu.VMEM((slow, kv_local, 3, rows, HD), f32),
            pltpu.VMEM((slow, kv_local, 3, rows, HD), f32),
            pltpu.VMEM((slow, kv_local, rows, HD), bf16),
            pltpu.VMEM((slow, kv_local, 2, rows), f32),
            pltpu.VMEM((kv_local, slow, nz, sub, HD), bf16),
            pltpu.VMEM((kv_local, slow, nz, 2, rows), f32),
            pltpu.VMEM((kv_local, 16, depth // kv_local), f32),
            pltpu.VMEM((nt, seq_rep, width), f32),
            pltpu.VMEM((nt - 1, seq_rep, width), bf16),
            pltpu.VMEM((nt - 1, seq_rep, width), bf16),
            pltpu.VMEM((seq_rep, LANES), f32),
            pltpu.VMEM((nt - 1, seq_rep, LANES), f32),
            dma((7,)),
            dma,
            dma((kv_local,)),
            dma((nz - 1,)),
            dma((nt - 1,)),
            dma((slow * kv_local,)),
            dma((kv_local,)),
            dma((kv_local,)),
            dma((7,)),
            dma,
            dma,
        ],
        compiler_params=pltpu.CompilerParams(
            collective_id=0, has_side_effects=True, vmem_limit_bytes=46 * 1024 * 1024
        ),
    )(
        block_counts,
        *(
            pltpu.with_memory_space_constraint(operand, pltpu.HBM)
            for operand in (
                lengths,
                slot_seq.reshape(1, slots),
                slot_block.reshape(1, slots),
                residual,
                queries,
                new_kv,
                norm_gain,
                kv_cache.reshape(tokens, kv_cache.shape[2]),
                out_weight,
            )
        ),
    )
    return (stream.astype(bf16), (stream * factor).astype(bf16))


def solution(mesh):
    placed = (
        P(("groups", "kvb"), None),
        P(("groups", "kvb"), "tp"),
        P(("groups", "kvb"), None),
        P(("groups", "kvb", "tp"), None, None),
        P("groups"),
        P(("groups", "kvb", "tp")),
        P(("groups", "kvb", "tp")),
        P(("groups", "kvb", "tp")),
        P("tp", None),
        P("tp"),
    )
    return jax.shard_map(
        on_device,
        mesh=mesh,
        in_specs=placed,
        out_specs=(P(("groups", "kvb"), "tp"), P(("groups", "kvb"), "tp")),
        check_vma=False,
    )
```

time: 32.8 us -> 29.4 us (0.90)
  Pallas kernels: 30.7 us -> 27.2 us
    pallas_call x1, Pallas kernels: 30.7 us -> 27.2 us  [on_device(): pl.pallas_call(body, out_shape=(jax.ShapeDtypeStruct((seq_rep, width), f3...]
where the time goes in v2:
time: 29.4 us; the launch traced here: 29.1 us
  Pallas kernels  27.2 us (93%)
  between operations  1.29 us (4%)
  other arithmetic  0.63 us (2%)
    pallas_call x1, Pallas kernels, on_device(): pl.pallas_call(body, out_shape=(jax.ShapeDtypeStruct((seq_rep, width), f3...  27.2 us
    convert_element_type x1, other arithmetic, on_device(): return (stream.astype(bf16), (stream * factor).astype(bf16))  0.63 us

profile of v2, /device:TPU:0, one launch (start us, length us, event | category | flops | bytes accessed | tf_op | source)
XLA Modules:
  0.0 29.1 jit_solution(6905169828871077438)
XLA Ops:
  1.3 27.2 %shard_map.113 = (f32[4,2048]{1,0:T(4,128)S(1)}, f32[4,2048]{1,0:T(4,128)S(1)}) custom-call(s32[1]{0:T(128)S(6)} %copy.12.refs_0_, s32[16]{0:T(128)} %refs_1_.1, s32[1,64]{1,0:T(1,128)} %bitcast.4, s32[1,64]{1,0:T(1,128)} %bitcast.5, bf16[4,8192]{1,0:T(4,128)(2,1)} %refs_4_.1, bf16[4,2048]{1,0:T(4,128)(2,1)} %refs_5_.1, bf16[4,2048]{1,0:T(4,128)(2,1)} %refs_6_.1, ...), custom_call_target="tpu_custom_call" | custom-call | tf_op jit(solution)/shard_map/pallas_call | solution.py:412
  28.5 0.6 %multiply_convert_fusion = (bf16[4,2048]{1,0:T(4,128)(2,1)}, bf16[4,2048]{1,0:T(4,128)(2,1)}) fusion(f32[4,2048]{1,0:T(4,128)S(1)} %get-tuple-element.4, f32[4,2048]{1,0:T(4,128)S(1)} %get-tuple-element.5), kind=kLoop, calls=%fused_computation | loop fusion | flops 24576 | bytes 98304 | tf_op jit(solution)/shard_map/convert_element_type | solution.py:479

commit v3 on v2

--- a/solution.py
+++ b/solution.py
@@ -77,8 +77,7 @@
     input_sem,
     cache_sem,
     weight_sem,
-    qz_recv,
-    qt_recv,
+    q_recv,
     pair_sem,
     zp_recv,
     zs_recv,
@@ -96,7 +95,7 @@
     slots = slot_seq_ref.shape[1]
     width = stream_ref.shape[1]
     slow = nt // CORES
-    QZ, QT, PAIR, ZP, ZS, RS, SQ = range(7)
+    QZ, QZ2, QT, PAIR, ZP, ZS, RS, SQ = range(8)
 
     def z_peer(a):
         return flipped(z, a)
@@ -107,10 +106,14 @@
     far_first = sorted(range(1, nt), key=lambda j: (j < CORES, j))
 
     barrier = pltpu.get_barrier_semaphore()
-    for a in range(1, nz):
-        pl.semaphore_signal(barrier, inc=1, device_id={"kvb": z_peer(a)}, device_id_type=MESH)
-    for j in range(1, nt):
-        pl.semaphore_signal(barrier, inc=1, device_id={"tp": tp_peer(j)}, device_id_type=MESH)
+    chips = [(jx, a) for jx in range(slow) for a in reversed(range(nz)) if jx or a]
+
+    def same_core(jx, a):
+        return {"kvb": z_peer(a), "tp": tp_peer(jx * CORES)}
+
+    for chip in chips:
+        pl.semaphore_signal(barrier, inc=1, device_id=same_core(*chip), device_id_type=MESH)
+    pl.semaphore_signal(barrier, inc=1, device_id={"tp": tp_peer(1)}, device_id_type=MESH)
 
     own = pl.ds(pl.multiple_of(t * width, LANES), width)
     inputs = [
@@ -141,7 +144,7 @@
     for k in range(kv_local):
         q_all[0, 0, k] = row_buf[k].astype(jnp.bfloat16)
     with jax.named_scope("barrier_wait"):
-        pl.semaphore_wait(barrier, nz - 1 + nt - 1)
+        pl.semaphore_wait(barrier, len(chips) + 1)
 
     def remote(src, dst, send, recv, target):
         pltpu.make_async_remote_copy(
@@ -156,14 +159,15 @@
     def wait_bytes(ref, sem):
         pltpu.make_async_copy(ref, ref, sem).wait()
 
-    for a in reversed(range(1, nz)):
-        remote(q_all.at[0, 0], q_all.at[0, a], QZ, qz_recv.at[a - 1], {"kvb": z_peer(a)})
-
-    def forward(a):
-        for j in far_first:
-            remote(q_all.at[0, a], q_all.at[j, a], QT, qt_recv.at[j - 1], {"tp": tp_peer(j)})
-
-    forward(0)
+    for jx, a in chips:
+        remote(q_all.at[0, 0], q_all.at[jx * CORES, a], QZ2 if jx else QZ, q_recv.at[jx * CORES], same_core(jx, a))
+
+    def await_queries(jx):
+        with jax.named_scope(f"q_wait{jx}"):
+            landed = q_all.at[0, pl.ds(1, nz - 1)] if jx == 0 else q_all.at[jx * CORES]
+            wait_bytes(landed, q_recv.at[jx * CORES])
+        j = jx * CORES + 1
+        remote(q_all.at[j - 1], q_all.at[j], QT, q_recv.at[j], {"tp": tp_peer(1)})
 
     depth = weight_buf.shape[0] // kv_local
     pieces = 4
@@ -209,20 +213,15 @@
     gain = gain_ref[...].astype(jnp.float32).reshape(1, width)
     wide_gain[...] = jnp.broadcast_to(gain, wide_gain.shape)
 
-    for a in range(1, nz):
-        with jax.named_scope(f"q_z_wait{a}"):
-            wait_bytes(q_all.at[0, a], qz_recv.at[a - 1])
-        forward(a)
-
+    await_queries(0)
     with jax.named_scope("cache_wait"):
         cache_copy.wait()
     lane = lax.broadcasted_iota(jnp.int32, (rows, LANES), 1)
     kept = {}
 
-    def attend(j, k):
+    def scores_of(j, k):
         first_kv = tp_peer(j) * local_heads // GROUP_HEADS
         key_at = pl.multiple_of((first_kv + k) * HD, LANES)
-        value_at = pl.multiple_of((KVH + first_kv + k) * HD, LANES)
         q_rows = q_all[j, :, k].reshape(rows, HD)
         scores = lax.dot_general(
             q_rows,
@@ -230,7 +229,11 @@
             (((1,), (1,)), ((), ())),
             preferred_element_type=jnp.float32,
         )
-        scores = scores * TOKEN_LOG2 + bias_buf[...]
+        return scores * TOKEN_LOG2 + bias_buf[...]
+
+    def attend(j, k, scores):
+        first_kv = tp_peer(j) * local_heads // GROUP_HEADS
+        value_at = pl.multiple_of((KVH + first_kv + k) * HD, LANES)
         peak = jnp.max(scores, axis=1, keepdims=True)
         weights = jnp.exp2(scores - jnp.maximum(peak, 0.1 * NEGATIVE))
         total = jnp.sum(weights, axis=1, keepdims=True)
@@ -280,11 +283,14 @@
     for jx in range(slow):
         for jc in range(CORES):
             j = jx * CORES + jc
-            if j > 0:
-                with jax.named_scope(f"q_tp_wait{j}"):
-                    wait_bytes(q_all.at[j], qt_recv.at[j - 1])
+            if jc:
+                with jax.named_scope(f"q_pair_wait{jx}"):
+                    wait_bytes(q_all.at[j], q_recv.at[j])
+            elif jx:
+                await_queries(jx)
+            scores = [scores_of(j, k) for k in range(kv_local)]
             for k in range(kv_local):
-                attend(j, k)
+                attend(j, k, scores[k])
                 if jc and jx:
                     join(jx, k)
         if jx == 0:
@@ -348,13 +354,15 @@
             remote(proj_send.at[j - 1], proj_recv.at[j - 1], RS, rs_recv, {"tp": tp_peer(j)})
     summed = residual_ref[...].astype(jnp.float32) + proj_sum[0]
     for ref, send in (
-        (q_all.at[0, pl.ds(1, nz - 1)], QZ),
-        (q_all.at[pl.ds(1, nt - 1)], QT),
+        (q_all.at[pl.ds(0, slow)], QT),
         (pair_send, PAIR),
         (z_part, ZP),
         (z_stat, ZS),
     ):
         wait_bytes(ref, send_sem.at[send])
+    wait_bytes(q_all.at[0, pl.ds(1, nz - 1)], send_sem.at[QZ])
+    if slow > 1:
+        wait_bytes(q_all.at[pl.ds(1, slow - 1)], send_sem.at[QZ2])
     with jax.named_scope("sum_wait"):
         wait_bytes(proj_recv, rs_recv)
     for j in range(1, nt):
@@ -447,12 +455,11 @@
             dma((7,)),
             dma,
             dma((kv_local,)),
-            dma((nz - 1,)),
-            dma((nt - 1,)),
+            dma((nt,)),
             dma((slow * kv_local,)),
             dma((kv_local,)),
             dma((kv_local,)),
-            dma((7,)),
+            dma((8,)),
             dma,
             dma,
         ],

time: 29.4 us -> 28.9 us (0.983)
  Pallas kernels: 27.2 us -> 26.8 us
    pallas_call x1, Pallas kernels: 27.2 us -> 26.8 us  [on_device(): pl.pallas_call(body, out_shape=(jax.ShapeDtypeStruct((seq_rep, width), f3...]
where the time goes in v3:
time: 28.9 us; the launch traced here: 28.7 us
  Pallas kernels  26.8 us (93%)
  between operations  1.29 us (4%)
  other arithmetic  0.63 us (2%)
    pallas_call x1, Pallas kernels, on_device(): pl.pallas_call(body, out_shape=(jax.ShapeDtypeStruct((seq_rep, width), f3...  26.8 us
    convert_element_type x1, other arithmetic, on_device(): return (stream.astype(bf16), (stream * factor).astype(bf16))  0.63 us

profile of v3, /device:TPU:0, one launch (start us, length us, event | category | flops | bytes accessed | tf_op | source)
XLA Modules:
  0.0 28.7 jit_solution(15506511414386178217)
XLA Ops:
  1.3 26.8 %shard_map.113 = (f32[4,2048]{1,0:T(4,128)S(1)}, f32[4,2048]{1,0:T(4,128)S(1)}) custom-call(s32[1]{0:T(128)S(6)} %copy.12.refs_0_, s32[16]{0:T(128)} %refs_1_.1, s32[1,64]{1,0:T(1,128)} %bitcast.4, s32[1,64]{1,0:T(1,128)} %bitcast.5, bf16[4,8192]{1,0:T(4,128)(2,1)} %refs_4_.1, bf16[4,2048]{1,0:T(4,128)(2,1)} %refs_5_.1, bf16[4,2048]{1,0:T(4,128)(2,1)} %refs_6_.1, ...), custom_call_target="tpu_custom_call" | custom-call | tf_op jit(solution)/shard_map/pallas_call | solution.py:420
  28.1 0.6 %multiply_convert_fusion = (bf16[4,2048]{1,0:T(4,128)(2,1)}, bf16[4,2048]{1,0:T(4,128)(2,1)}) fusion(f32[4,2048]{1,0:T(4,128)S(1)} %get-tuple-element.4, f32[4,2048]{1,0:T(4,128)S(1)} %get-tuple-element.5), kind=kLoop, calls=%fused_computation | loop fusion | flops 24576 | bytes 98304 | tf_op jit(solution)/shard_map/convert_element_type | solution.py:486

commit v4 on v3

--- a/solution.py
+++ b/solution.py
@@ -17,6 +17,7 @@
 EPSILON = 1e-06
 LANES = 128
 CORES = 2
+TILE = 8
 TOKEN_LOG2 = math.log2(math.e) * HD ** (-0.5)
 MESH = pl.DeviceIdType.MESH
 
@@ -68,7 +69,9 @@
     z_stat_send,
     z_part,
     z_stat,
-    lhs_buf,
+    fresh_buf,
+    fresh_values,
+    chosen_buf,
     proj_sum,
     proj_send,
     proj_recv,
@@ -135,6 +138,13 @@
     cache_copy = pltpu.make_async_copy(cache_ref, cache_buf, cache_sem)
     cache_copy.start()
     inputs[0].wait()
+    depth = weight_buf.shape[0] // kv_local
+    pieces = 4
+    for i in range(kv_local * pieces):
+        part_rows = pl.ds(i * (depth // pieces), depth // pieces)
+        pltpu.make_async_copy(
+            weight_ref.at[part_rows, :], weight_buf.at[part_rows, :], weight_sem.at[i // pieces]
+        ).start()
 
     wide_q = queries_ref[...].astype(jnp.float32)
     for k in range(kv_local):
@@ -169,13 +179,6 @@
         j = jx * CORES + 1
         remote(q_all.at[j - 1], q_all.at[j], QT, q_recv.at[j], {"tp": tp_peer(1)})
 
-    depth = weight_buf.shape[0] // kv_local
-    pieces = 4
-    for i in range(kv_local * pieces):
-        part_rows = pl.ds(i * (depth // pieces), depth // pieces)
-        pltpu.make_async_copy(
-            weight_ref.at[part_rows, :], weight_buf.at[part_rows, :], weight_sem.at[i // pieces]
-        ).start()
     for copy in inputs[1:]:
         copy.wait()
 
@@ -201,15 +204,22 @@
     bias_buf[...] = jnp.where(offset < reach, 0.0, NEGATIVE)
 
     own_kv = t * local_heads // GROUP_HEADS
-    fresh = []
     for k in range(kv_local):
         for part in range(2):
             at = pl.multiple_of((part * KVH + own_kv + k) * HD, LANES)
             piece = new_kv_ref[:, pl.ds(at, HD)].astype(jnp.float32)
             for q in range(per_kv):
                 new_buf[k, part, q * seq_rep : (q + 1) * seq_rep, :] = piece
-        fresh.append(jnp.sum(row_buf[k] * new_buf[k, 0], axis=1, keepdims=True) * TOKEN_LOG2)
-    lhs_buf[...] = jnp.zeros_like(lhs_buf)
+        fresh = jnp.sum(row_buf[k] * new_buf[k, 0], axis=1, keepdims=True) * TOKEN_LOG2
+        fresh = jnp.concatenate([fresh] * nz, axis=0)
+        fresh_buf[k] = jnp.broadcast_to(fresh, (rows, LANES)).T[:8]
+        blank = jnp.zeros((rows - sub, HD), jnp.float32)
+        fresh_values[k] = jnp.concatenate([new_buf[k, 1], blank], axis=0).astype(jnp.bfloat16)
+    out_row = lax.broadcasted_iota(jnp.int32, chosen_buf.shape, 0)
+    in_row = lax.rem(lax.broadcasted_iota(jnp.int32, chosen_buf.shape, 1), sub)
+    out_seq = lax.rem(out_row, TILE)
+    chosen = (out_seq < seq_rep) & (in_row == out_row // TILE * seq_rep + out_seq)
+    chosen_buf[...] = chosen.astype(jnp.float32)
     gain = gain_ref[...].astype(jnp.float32).reshape(1, width)
     wide_gain[...] = jnp.broadcast_to(gain, wide_gain.shape)
 
@@ -297,61 +307,75 @@
             for k in range(kv_local):
                 join(jx, k)
 
-    def columns_of(pieces):
-        height = -(-len(pieces) // 8) * 8
-        index = lax.broadcasted_iota(jnp.int32, (height, rows), 0)
-        tile = jnp.zeros((height, rows), jnp.float32)
-        for i, piece in enumerate(pieces):
-            tile = jnp.where(index == i, piece, tile)
-        return tile.T
-
-    sources = [(jx, a) for jx in range(slow) for a in range(nz)]
-    for k in range(kv_local):
+    def over_sources(row, pick):
+        turned = [pltpu.roll(row, a * sub, 1) for a in range(1, nz)]
+        for other in turned:
+            row = pick(row, other)
+        return row
+
+    def attended_of(k):
         with jax.named_scope(f"z_wait{k}"):
+            wait_bytes(z_stat.at[k], zs_recv.at[k])
             wait_bytes(z_part.at[k], zp_recv.at[k])
-            wait_bytes(z_stat.at[k], zs_recv.at[k])
-        spread_stat = columns_of([z_stat[k, jx, a, i : i + 1, :] for jx, a in sources for i in range(2)])
-        peaks, sums = (
-            [
-                spread_stat[a * sub : (a + 1) * sub, 2 * n + i : 2 * n + i + 1]
-                for n, (_, a) in enumerate(sources)
-            ]
-            for i in range(2)
-        )
-        top = fresh[k]
+        peaks, sums = ([stat_row(k, jx, i) for jx in range(slow)] for i in range(2))
+        own_score = fresh_buf[k]
+        top = own_score
         for piece in peaks:
             top = jnp.maximum(top, piece)
-        denominator = jnp.exp2(fresh[k] - top)
-        numerator = denominator * new_buf[k, 1]
-        for n, (jx, a) in enumerate(sources):
-            scale = jnp.exp2(peaks[n] - top)
-            denominator += scale * sums[n]
-            numerator += scale * z_part[k, jx, a].astype(jnp.float32)
-        row_buf[k] = numerator / denominator
-        for q in range(per_kv):
-            lhs_buf[k, 0:seq_rep, q * HD : (q + 1) * HD] = row_buf[
-                k, q * seq_rep : (q + 1) * seq_rep, :
-            ]
-        attended = lhs_buf[k].astype(jnp.bfloat16)
+        top = over_sources(top, jnp.maximum)
+        scales = [jnp.exp2(piece - top) for piece in peaks]
+        denominator = sum(scale * piece for scale, piece in zip(scales, sums))
+        own_scale = jnp.exp2(own_score - top)
+        inverse = 1.0 / (over_sources(denominator, jnp.add) + own_scale)
+        total = jnp.zeros((per_kv * TILE, HD), jnp.float32)
+        blocks = [z_part[k, jx].reshape(rows, HD) for jx in range(slow)] + [fresh_values[k]]
+        factors = [scale * inverse for scale in scales] + [own_scale * inverse]
+        for n in range(0, slow + 1, 2):
+            wide = jnp.concatenate(
+                [
+                    chosen_buf[...] * jnp.broadcast_to(factor[0:1], chosen_buf.shape)
+                    for factor in factors[n : n + 2]
+                ],
+                axis=1,
+            )
+            high = wide.astype(jnp.bfloat16)
+            low = (wide - high.astype(jnp.float32)).astype(jnp.bfloat16)
+            block = jnp.concatenate(blocks[n : n + 2], axis=0)
+            total += jnp.dot(high, block, preferred_element_type=jnp.float32)
+            total += jnp.dot(low, block, preferred_element_type=jnp.float32)
+        line = jnp.concatenate([total[q * TILE : (q + 1) * TILE] for q in range(per_kv)], axis=1)
+        return jnp.concatenate([line, jnp.zeros_like(line)], axis=0).astype(jnp.bfloat16)
+
+    def stat_row(k, jx, i):
+        row = jnp.zeros((8, rows), jnp.float32)
+        row_lane = lax.broadcasted_iota(jnp.int32, (8, rows), 1) // sub
+        for a in range(nz):
+            row = jnp.where(row_lane == a, z_stat[k, jx, a, i : i + 1, :], row)
+        return row
+
+    def project(k, j):
+        column = pl.ds(pl.multiple_of(tp_peer(j) * width, LANES), width)
+        return jnp.dot(
+            attended[k],
+            weight_buf[k * depth : (k + 1) * depth, column],
+            preferred_element_type=jnp.float32,
+        )[:seq_rep]
+
+    def send_block(j):
+        proj_send[j - 1] = proj_sum[j].astype(jnp.bfloat16)
+        remote(proj_send.at[j - 1], proj_recv.at[j - 1], RS, rs_recv, {"tp": tp_peer(j)})
+
+    for k in range(kv_local):
         with jax.named_scope(f"weight_wait{k}"):
             half = pl.ds(k * depth, depth)
             pltpu.make_async_copy(
                 weight_ref.at[half, :], weight_buf.at[half, :], weight_sem.at[k]
             ).wait()
-        for j in far_first + [0]:
-            column = pl.ds(pl.multiple_of(tp_peer(j) * width, LANES), width)
-            got = jnp.dot(
-                attended,
-                weight_buf[k * depth : (k + 1) * depth, column],
-                preferred_element_type=jnp.float32,
-            )[:seq_rep]
-            if k > 0:
-                got += proj_sum[j]
-            if j == 0 or k < kv_local - 1:
-                proj_sum[j] = got
-                continue
-            proj_send[j - 1] = got.astype(jnp.bfloat16)
-            remote(proj_send.at[j - 1], proj_recv.at[j - 1], RS, rs_recv, {"tp": tp_peer(j)})
+    attended = [attended_of(k) for k in range(kv_local)]
+    for j in far_first + [0]:
+        proj_sum[j] = sum(project(k, j) for k in range(kv_local))
+        if j > 0:
+            send_block(j)
     summed = residual_ref[...].astype(jnp.float32) + proj_sum[0]
     for ref, send in (
         (q_all.at[pl.ds(0, slow)], QT),
@@ -446,7 +470,9 @@
             pltpu.VMEM((slow, kv_local, 2, rows), f32),
             pltpu.VMEM((kv_local, slow, nz, sub, HD), bf16),
             pltpu.VMEM((kv_local, slow, nz, 2, rows), f32),
-            pltpu.VMEM((kv_local, 16, depth // kv_local), f32),
+            pltpu.VMEM((kv_local, 8, rows), f32),
+            pltpu.VMEM((kv_local, rows, HD), bf16),
+            pltpu.VMEM((sub // seq_rep * TILE, rows), f32),
             pltpu.VMEM((nt, seq_rep, width), f32),
             pltpu.VMEM((nt - 1, seq_rep, width), bf16),
             pltpu.VMEM((nt - 1, seq_rep, width), bf16),

time: 28.9 us -> 27.6 us (0.955)
  Pallas kernels: 26.8 us -> 25.4 us
    pallas_call x1, Pallas kernels: 26.8 us -> 25.4 us  [on_device(): pl.pallas_call(body, out_shape=(jax.ShapeDtypeStruct((seq_rep, width), f3...]
where the time goes in v4:
time: 27.6 us; the launch traced here: 27.3 us
  Pallas kernels  25.4 us (92%)
  between operations  1.29 us (5%)
  other arithmetic  0.63 us (2%)
    pallas_call x1, Pallas kernels, on_device(): pl.pallas_call(body, out_shape=(jax.ShapeDtypeStruct((seq_rep, width), f3...  25.4 us
    convert_element_type x1, other arithmetic, on_device(): return (stream.astype(bf16), (stream * factor).astype(bf16))  0.63 us

profile of v4, /device:TPU:0, one launch (start us, length us, event | category | flops | bytes accessed | tf_op | source)
XLA Modules:
  0.0 27.3 jit_solution(11638097339552046904)
XLA Ops:
  1.3 25.4 %shard_map.113 = (f32[4,2048]{1,0:T(4,128)S(1)}, f32[4,2048]{1,0:T(4,128)S(1)}) custom-call(s32[1]{0:T(128)S(6)} %copy.12.refs_0_, s32[16]{0:T(128)} %refs_1_.1, s32[1,64]{1,0:T(1,128)} %bitcast.4, s32[1,64]{1,0:T(1,128)} %bitcast.5, bf16[4,8192]{1,0:T(4,128)(2,1)} %refs_4_.1, bf16[4,2048]{1,0:T(4,128)(2,1)} %refs_5_.1, bf16[4,2048]{1,0:T(4,128)(2,1)} %refs_6_.1, ...), custom_call_target="tpu_custom_call" | custom-call | tf_op jit(solution)/shard_map/pallas_call | solution.py:444
  26.7 0.6 %multiply_convert_fusion = (bf16[4,2048]{1,0:T(4,128)(2,1)}, bf16[4,2048]{1,0:T(4,128)(2,1)}) fusion(f32[4,2048]{1,0:T(4,128)S(1)} %get-tuple-element.4, f32[4,2048]{1,0:T(4,128)S(1)} %get-tuple-element.5), kind=kLoop, calls=%fused_computation | loop fusion | flops 24576 | bytes 98304 | tf_op jit(solution)/shard_map/convert_element_type | solution.py:512
